TPU v7x, 32 devices: a whole 2x2x4 slice. The times are simulated.
32 devices in a mesh: win: 4 (over z), slab: 8 (over y, x, core).
Axes of the slice: x: 2, y: 2, z: 4, core: 2. Of those that a mesh axis runs over, the one named last changes fastest.
Arguments:
- lambdas: float32 [16], P('win'), parts along dimension 0, may hold values from 0 to 1
- charge_a: float32 [16, 4096], P('win', 'slab'), parts along dimension 0, may hold values from -3 to 3
- charge_b: float32 [16, 4096], P('win', 'slab'), parts along dimension 0, may hold values from -3 to 3
- perturbed: int32 [16, 4096], P('win', 'slab'), parts along dimension 0, may hold values 0 or 1
- grid_index: int32 [3, 16, 4096], P(None, 'win', 'slab'), parts along dimension 1, may hold values from 0 to 127, as said below
- spline_weights: float32 [3, 4, 16, 4096], P(None, None, 'win', 'slab'), parts along dimension 2, may hold values from 0 to 1, as said below
- spline_slopes: float32 [3, 4, 16, 4096], P(None, None, 'win', 'slab'), parts along dimension 2, may hold values from -1 to 1, as said below
Outputs:
- forces: float32 [3, 16, 4096], P(None, 'win', 'slab'), parts along dimension 1
- energy: float32 [16], P('win'), parts along dimension 0
- lambda_slope: float32 [16], P('win'), parts along dimension 0
There are 4 independent parts, one for each index of `win`. A program takes and returns all parts, laid end to end along the dimension named above; each array names one. Nothing has to cross between parts.
Inputs may be any that keep to these rules, and one draw needn't show every extreme that they name: `grid_index`: the z index of atom i lies in the planes of the slab index that holds it: from (i // 512) * 16 to that plus 16 - 1. `spline_weights`: along each dimension the four weights are the cubic B-spline values (1-u)^3/6, (3u^3-6u^2+4)/6, (-3u^3+3u^2+3u+1)/6, u^3/6 of the atom's fractional offset u in [0, 1). `spline_slopes`: the derivatives in u of spline_weights at the same offsets.
All inputs are finite; a program needn't handle non-finite values. No bound on the sum of `perturbed` on one device may be relied on, other than what follows from the above.
Results may differ from a plain program's by a relative error of at most 0.0003.
Values sent between devices are 32-bit elements; how exact they have to be, the bound alone decides.
A program may use at most 64 MiB of HBM per device.

v0:
```python
import math
import jax
import jax.numpy as jnp
from jax import lax
from jax.sharding import PartitionSpec as P

NX = 128
NY = 128
NZ = 128
highest = lax.Precision.HIGHEST
gauss_width = 2.0


def passed_along(value, axis, steps):
    count = lax.axis_size(axis)
    pairs = [(source, (source + steps) % count) for source in range(count)]
    return lax.ppermute(value, axis, pairs)


def dft_tables(length):
    counter = jnp.arange(length, dtype=jnp.int32)
    product = counter[:, None] * counter[None, :] % length
    angles = product.astype(jnp.float32) * (2.0 * math.pi / length)
    return (jnp.cos(angles), jnp.sin(angles))


def frequency(counter, length):
    return jnp.where(counter >= length // 2, counter - length, counter).astype(jnp.float32) / length


def stencil_table(first_cell, weights, length):
    grid_cells = jnp.arange(length, dtype=jnp.int32)
    matrix = jnp.zeros((first_cell.shape[0], length), jnp.float32)
    for offset in range(4):
        target = (first_cell + offset) % length
        matrix = matrix + weights[offset][:, None] * (
            grid_cells[None, :] == target[:, None]
        ).astype(jnp.float32)
    return matrix


def plane_table(first_cell, weights, plane_count):
    planes = jnp.arange(plane_count, dtype=jnp.int32)
    matrix = jnp.zeros((plane_count, first_cell.shape[0]), jnp.float32)
    for offset in range(4):
        matrix = matrix + weights[offset][None, :] * (
            planes[:, None] == (first_cell + offset)[None, :]
        ).astype(jnp.float32)
    return matrix


def spread_block(charge, cell_index, weights, first_plane, plane_count):
    rows_x = stencil_table(cell_index[0], weights[0], NX)
    rows_y = stencil_table(cell_index[1], weights[1], NY)
    depth_table = plane_table(cell_index[2] - first_plane, weights[2], plane_count)
    right_side = (depth_table * charge[None, :]).T[:, :, None] * rows_y[:, None, :]
    return jnp.einsum("ia,ipb->pab", rows_x, right_side, precision=highest)


def sample_block(
    charge, charge_step, cell_index, weights, slopes, values, first_plane, plane_count
):
    rows_x = stencil_table(cell_index[0], weights[0], NX)
    steep_x = stencil_table(cell_index[0], slopes[0], NX)
    rows_y = stencil_table(cell_index[1], weights[1], NY)
    steep_y = stencil_table(cell_index[1], slopes[1], NY)
    depth_table = plane_table(cell_index[2] - first_plane, weights[2], plane_count)
    steep_z = plane_table(cell_index[2] - first_plane, slopes[2], plane_count)
    along_rows = jnp.einsum("pab,ib->ipa", values, rows_y, precision=highest)
    reduced = jnp.einsum("ia,ipa->ip", rows_x, along_rows, precision=highest)
    reduced_dx = jnp.einsum("ia,ipa->ip", steep_x, along_rows, precision=highest)
    along_steep = jnp.einsum("pab,ib->ipa", values, steep_y, precision=highest)
    reduced_dy = jnp.einsum("ia,ipa->ip", rows_x, along_steep, precision=highest)
    sampled = jnp.einsum("pi,ip->i", depth_table, reduced, precision=highest)
    force_x = -charge * jnp.einsum("pi,ip->i", depth_table, reduced_dx, precision=highest)
    force_y = -charge * jnp.einsum("pi,ip->i", depth_table, reduced_dy, precision=highest)
    force_z = -charge * jnp.einsum("pi,ip->i", steep_z, reduced, precision=highest)
    return (jnp.stack([force_x, force_y, force_z]), jnp.sum(charge_step * sampled))


def xy_forward(owned_grid, planar):
    cosine_x, sine_x, cosine_y, sine_y = planar
    part_real = jnp.einsum("ka,wpab->wpkb", cosine_x, owned_grid, precision=highest)
    part_imaginary = -jnp.einsum("ka,wpab->wpkb", sine_x, owned_grid, precision=highest)
    plane_real = jnp.einsum("wpkb,bl->wpkl", part_real, cosine_y, precision=highest) + jnp.einsum(
        "wpkb,bl->wpkl", part_imaginary, sine_y, precision=highest
    )
    plane_imaginary = jnp.einsum(
        "wpkb,bl->wpkl", part_imaginary, cosine_y, precision=highest
    ) - jnp.einsum("wpkb,bl->wpkl", part_real, sine_y, precision=highest)
    return jnp.stack([plane_real, plane_imaginary], axis=1)


def xy_inverse(slab_values, planar):
    cosine_x, sine_x, cosine_y, sine_y = planar
    value_real = slab_values[:, 0]
    value_imaginary = slab_values[:, 1]
    half_real = jnp.einsum("wpkl,lb->wpkb", value_real, cosine_y, precision=highest) - jnp.einsum(
        "wpkl,lb->wpkb", value_imaginary, sine_y, precision=highest
    )
    half_imaginary = jnp.einsum(
        "wpkl,lb->wpkb", value_imaginary, cosine_y, precision=highest
    ) + jnp.einsum("wpkl,lb->wpkb", value_real, sine_y, precision=highest)
    return jnp.einsum("ak,wpkb->wpab", cosine_x, half_real, precision=highest) - jnp.einsum(
        "ak,wpkb->wpab", sine_x, half_imaginary, precision=highest
    )


def influence_block(first_column, column_count):
    freq_z = frequency(jnp.arange(NZ, dtype=jnp.int32), NZ)[:, None, None]
    freq_x = frequency(first_column + jnp.arange(column_count, dtype=jnp.int32), NX)[None, :, None]
    freq_y = frequency(jnp.arange(NY, dtype=jnp.int32), NY)[None, None, :]
    squared = freq_z * freq_z + freq_x * freq_x + freq_y * freq_y
    positive = squared > 0
    safe_value = jnp.where(positive, squared, jnp.float32(1.0))
    return jnp.where(
        positive,
        jnp.exp(-gauss_width * squared) / (math.pi * NX * NY * NZ * safe_value),
        jnp.float32(0.0),
    )


def column_transform(columns, influence, cosine_z, sine_z):
    column_real = columns[:, 0]
    column_imaginary = columns[:, 1]
    depth_real = jnp.einsum("kz,nzab->nkab", cosine_z, column_real, precision=highest) + jnp.einsum(
        "kz,nzab->nkab", sine_z, column_imaginary, precision=highest
    )
    depth_imaginary = jnp.einsum(
        "kz,nzab->nkab", cosine_z, column_imaginary, precision=highest
    ) - jnp.einsum("kz,nzab->nkab", sine_z, column_real, precision=highest)
    energy_part = 0.5 * jnp.sum(
        influence * (depth_real * depth_real + depth_imaginary * depth_imaginary), axis=(1, 2, 3)
    )
    scaled_real = influence * depth_real
    scaled_imaginary = influence * depth_imaginary
    back_real = jnp.einsum("zk,nkab->nzab", cosine_z, scaled_real, precision=highest) - jnp.einsum(
        "zk,nkab->nzab", sine_z, scaled_imaginary, precision=highest
    )
    back_imaginary = jnp.einsum(
        "zk,nkab->nzab", cosine_z, scaled_imaginary, precision=highest
    ) + jnp.einsum("zk,nkab->nzab", sine_z, scaled_real, precision=highest)
    return (jnp.stack([back_real, back_imaginary], axis=1), energy_part)


def body(lambdas, charge_a, charge_b, perturbed, grid_index, spline_weights, spline_slopes):
    atoms_here = charge_a.shape[1]
    slab_count = lax.axis_size("slab")
    slab_depth = NZ // slab_count
    flag_values = perturbed.astype(jnp.float32)
    charges = charge_a + flag_values * lambdas[:, None] * (charge_b - charge_a)
    charge_steps = flag_values * (charge_b - charge_a)
    weight_windows = jnp.moveaxis(spline_weights, 2, 0)
    slope_windows = jnp.moveaxis(spline_slopes, 2, 0)
    index_windows = jnp.moveaxis(grid_index, 1, 0)
    cosine_x, sine_x = dft_tables(NX)
    cosine_y, sine_y = dft_tables(NY)
    cosine_z, sine_z = dft_tables(NZ)
    planar = (cosine_x, sine_x, cosine_y, sine_y)
    plane_count = slab_depth + 3
    column_count = NX // slab_count
    first_plane = lax.axis_index("slab") * slab_depth

    def spread_window(inputs):
        return spread_block(inputs[0], inputs[1], inputs[2], first_plane, plane_count)

    extended = lax.map(spread_window, (charges, index_windows, weight_windows))
    reach_count = (slab_depth + 2) // slab_depth
    owned_grid = extended[:, :slab_depth]
    for distance in range(1, reach_count + 1):
        last_plane = min(plane_count, (distance + 1) * slab_depth)
        arrived = passed_along(extended[:, distance * slab_depth : last_plane], "slab", distance)
        owned_grid = owned_grid + jnp.pad(
            arrived, ((0, 0), (0, slab_depth - arrived.shape[1]), (0, 0), (0, 0))
        )
    slab_spectrum = xy_forward(owned_grid, planar)
    influence = influence_block(lax.axis_index("slab") * column_count, column_count)
    stacked, energy_part = column_transform(
        lax.all_to_all(slab_spectrum, "slab", split_axis=3, concat_axis=2, tiled=True),
        influence,
        cosine_z,
        sine_z,
    )
    slab_values = lax.all_to_all(stacked, "slab", split_axis=2, concat_axis=3, tiled=True)
    slab_values, energy_part = (slab_values, energy_part)
    potential = xy_inverse(slab_values, planar)
    pieces = [potential]
    for distance in range(1, reach_count + 1):
        depth_taken = min(slab_depth, plane_count - distance * slab_depth)
        pieces.append(passed_along(potential[:, :depth_taken], "slab", -distance))
    potential_field = jnp.concatenate(pieces, axis=1)

    def sample_window(inputs):
        charge, charge_step, cell_index, weights, slopes, values = inputs
        return sample_block(
            charge, charge_step, cell_index, weights, slopes, values, first_plane, plane_count
        )

    window_forces, derivative_part = lax.map(
        sample_window,
        (charges, charge_steps, index_windows, weight_windows, slope_windows, potential_field),
    )
    forces = jnp.moveaxis(window_forces, 0, 1)
    energy_total = lax.psum(energy_part, "slab")
    derivative_total = lax.psum(derivative_part, "slab")
    atom_total = atoms_here * slab_count
    return (forces, energy_total / atom_total, derivative_total / atom_total)


def solution(mesh):
    return jax.shard_map(
        body,
        mesh=mesh,
        in_specs=(
            P("win"),
            P("win", "slab"),
            P("win", "slab"),
            P("win", "slab"),
            P(None, "win", "slab"),
            P(None, None, "win", "slab"),
            P(None, None, "win", "slab"),
        ),
        out_specs=(P(None, "win", "slab"), P("win"), P("win")),
        check_vma=False,
    )
```

profile of v0, /device:TPU:0, one launch (start us, length us, event | category | flops | bytes accessed | tf_op | source)
XLA Modules:
  0.0 637.9 jit_solution(1168671799262427273)
XLA Ops:
  3.1 25.3 %while.26 = (s32[]{:T(128)}, f32[4,19,128,128]{2,3,1,0:T(8,128)}, s32[4,3,512]{2,1,0:T(4,128)S(1)}, s32[]{:T(128)}, f32[4,3,4,512]{3,2,1,0:T(4,128)S(1)}, /*inde...) while((s32[]{:T(128)}, f32[4,19,128,128]{2,3,1,0:T(8,128)}, ...), condition=%wide.region_1.2_spmd, body=%wide.region_0.1_spmd.sunk | while | flops 1915456512 | bytes 2517685 | solution.py:167
  30.7 12.5 %collective-permute-done = f32[4,3,128,128]{2,3,1,0:T(8,128)S(1)} collective-permute-done((f32[4,3,128,128]{2,3,1,0:T(8,128)S(1)}, f32[4,3,128,128]{2,3,1,0:T(8,128)S(1)}, u32[]{:S(2)}, u32[]{:S(2)}) %collective-permute-start) | collective-permute-done | bytes 786464 | tf_op jit(solution)/shard_map/ppermute | solution.py:17
  56.2 7.4 %fusion.108 = f32[4,16,128,128]{3,2,1,0:T(8,128)S(1)} fusion(f32[4,16,128,128]{3,2,1,0:T(8,128)S(1)} %fusion.130), kind=kOutput, calls=%fused_computation.248 | convolution fusion | flops 1611890688 | bytes 8388608 | tf_op jit(solution)/shard_map/wpkb,bl->wpkl/dot_general | solution.py:88
  67.6 7.5 %add_bitcast_fusion.3 = f32[4,1,16,128,128]{4,3,2,0,1:T(8,128)S(1)} fusion(f32[4,16,128,128]{3,2,1,0:T(8,128)S(1)} %fusion.110, f32[4,16,128,128]{3,2,1,0:T(8,128)S(1)} %fusion.131), kind=kOutput, calls=%fused_computation.264 | convolution fusion | flops 1611890688 | bytes 12582912 | tf_op jit(solution)/shard_map/wpkb,bl->wpkl/dot_general | solution.py:85
  83.3 8.1 %copy.64 = f32[4,2,16,128,128]{4,2,0,1,3:T(8,128)} copy(f32[4,2,16,128,128]{4,3,2,0,1:T(8,128)S(1)} %pad_maximum_fusion) | data formatting | bytes 16777216 | tf_op jit(solution)/shard_map/stack | solution.py:91
  97.1 93.5 %all-to-all-done = f32[4,2,16,128,128]{4,2,0,1,3:T(8,128)} async-done(((f32[4,2,16,128,128]{4,2,0,1,3:T(8,128)}), f32[4,2,16,128,128]{4,2,0,1,3:T(8,128)}, u32[]{:S(2)}, u32[]{:S(2)}) %all-to-all-start) | async-done | bytes 8388640 | tf_op jit(solution)/shard_map/all_to_all | solution.py:179
  190.6 8.2 %copy.66 = f32[4,2,8,16,16,128]{5,4,3,2,1,0:T(8,128)S(1)} copy(f32[4,2,8,16,16,128]{5,3,0,1,4,2:T(8,128)} %bitcast.86) | data formatting | bytes 16777216 | tf_op jit(solution)/shard_map/all_to_all | solution.py:179
  257.7 10.3 %copy.69 = f32[4,2,128,16,128]{4,3,0,1,2:T(8,128)} copy(f32[4,2,128,16,128]{2,4,3,0,1:T(8,128)} %pad_maximum_fusion.1) | data formatting | bytes 16777216 | tf_op jit(solution)/shard_map/stack | solution.py:143
  267.9 97.8 %all_to_all.36 = f32[4,2,128,16,128]{4,3,0,1,2:T(8,128)S(1)} all-to-all(f32[4,2,128,16,128]{4,3,0,1,2:T(8,128)} %copy.69), channel_id=1, replica_groups=mesh['win'=4,'slab'=8] {'slab'}, dimensions={2} | all-to-all | bytes 16777216 | tf_op jit(solution)/shard_map/all_to_all | solution.py:184
  399.1 9.4 %collective-permute-done.1 = f32[4,3,128,128]{2,3,1,0:T(8,128)S(1)} collective-permute-done((f32[4,3,128,128]{2,3,1,0:T(8,128)S(1)}, f32[4,3,128,128]{2,3,1,0:T(8,128)S(1)}, u32[]{:S(2)}, u32[]{:S(2)}) %collective-permute-start.1) | collective-permute-done | bytes 786464 | tf_op jit(solution)/shard_map/ppermute | solution.py:17
  413.5 209.0 %while.27 = (s32[]{:T(128)}, f32[4,3,512]{2,0,1:T(4,128)S(1)}, f32[4]{0:T(128)S(1)}, f32[4,512]{1,0:T(4,128)}, s32[4,3,512]{2,1,0:T(4,128)S(1)}, /*index=5*/s32[...) while((s32[]{:T(128)}, f32[4,3,512]{2,0,1:T(4,128)S(1)}, ...), condition=%wide.region_4.5_spmd, body=%wide.region_2.4_spmd.sunk | while | flops 3872960512 | bytes 29543656 | solution.py:199
  420.7 11.9 %fusion.328 = f32[512,1,19]{2,1,0:T(1,128)S(1)} fusion(f32[512,128,1]{1,2,0:T(1,128)S(1)} %bitcast.372, f32[512,19,128]{2,0,1:T(8,128)S(1)} %fusion.327), kind=kOutput, calls=%fused_computation.94.clone.1 | convolution fusion | flops 14942208 | bytes 5281792 | tf_op jit(solution)/shard_map/while/body/eval_jaxpr/ia,ipa->ip/dot_general | solution.py:73
  438.5 12.1 %fusion.329 = f32[512,1,19]{2,1,0:T(1,128)S(1)} fusion(f32[512,128,1]{1,2,0:T(1,128)S(1)} %bitcast.379, f32[512,19,128]{2,0,1:T(8,128)S(1)} %fusion.325), kind=kOutput, calls=%fused_computation.92.clone.1 | convolution fusion | flops 14942208 | bytes 5281792 | tf_op jit(solution)/shard_map/while/body/eval_jaxpr/ia,ipa->ip/dot_general | solution.py:71
  450.6 11.9 %fusion.326 = f32[512,1,19]{2,1,0:T(1,128)S(1)} fusion(f32[512,128,1]{1,2,0:T(1,128)S(1)} %bitcast.373, f32[512,19,128]{2,0,1:T(8,128)S(1)} %fusion.325), kind=kOutput, calls=%fused_computation.90.clone.1 | convolution fusion | flops 14942208 | bytes 5281792 | tf_op jit(solution)/shard_map/while/body/eval_jaxpr/ia,ipa->ip/dot_general | solution.py:70
  472.6 12.1 %fusion.328 = f32[512,1,19]{2,1,0:T(1,128)S(1)} fusion(f32[512,128,1]{1,2,0:T(1,128)S(1)} %bitcast.372, f32[512,19,128]{2,0,1:T(8,128)S(1)} %fusion.327), kind=kOutput, calls=%fused_computation.94.clone.1 | convolution fusion | flops 14942208 | bytes 5281792 | tf_op jit(solution)/shard_map/while/body/eval_jaxpr/ia,ipa->ip/dot_general | solution.py:73
  490.7 11.9 %fusion.329 = f32[512,1,19]{2,1,0:T(1,128)S(1)} fusion(f32[512,128,1]{1,2,0:T(1,128)S(1)} %bitcast.379, f32[512,19,128]{2,0,1:T(8,128)S(1)} %fusion.325), kind=kOutput, calls=%fused_computation.92.clone.1 | convolution fusion | flops 14942208 | bytes 5281792 | tf_op jit(solution)/shard_map/while/body/eval_jaxpr/ia,ipa->ip/dot_general | solution.py:71
  502.5 11.9 %fusion.326 = f32[512,1,19]{2,1,0:T(1,128)S(1)} fusion(f32[512,128,1]{1,2,0:T(1,128)S(1)} %bitcast.373, f32[512,19,128]{2,0,1:T(8,128)S(1)} %fusion.325), kind=kOutput, calls=%fused_computation.90.clone.1 | convolution fusion | flops 14942208 | bytes 5281792 | tf_op jit(solution)/shard_map/while/body/eval_jaxpr/ia,ipa->ip/dot_general | solution.py:70
  524.7 11.9 %fusion.328 = f32[512,1,19]{2,1,0:T(1,128)S(1)} fusion(f32[512,128,1]{1,2,0:T(1,128)S(1)} %bitcast.372, f32[512,19,128]{2,0,1:T(8,128)S(1)} %fusion.327), kind=kOutput, calls=%fused_computation.94.clone.1 | convolution fusion | flops 14942208 | bytes 5281792 | tf_op jit(solution)/shard_map/while/body/eval_jaxpr/ia,ipa->ip/dot_general | solution.py:73
  542.6 11.9 %fusion.329 = f32[512,1,19]{2,1,0:T(1,128)S(1)} fusion(f32[512,128,1]{1,2,0:T(1,128)S(1)} %bitcast.379, f32[512,19,128]{2,0,1:T(8,128)S(1)} %fusion.325), kind=kOutput, calls=%fused_computation.92.clone.1 | convolution fusion | flops 14942208 | bytes 5281792 | tf_op jit(solution)/shard_map/while/body/eval_jaxpr/ia,ipa->ip/dot_general | solution.py:71
  554.5 12.1 %fusion.326 = f32[512,1,19]{2,1,0:T(1,128)S(1)} fusion(f32[512,128,1]{1,2,0:T(1,128)S(1)} %bitcast.373, f32[512,19,128]{2,0,1:T(8,128)S(1)} %fusion.325), kind=kOutput, calls=%fused_computation.90.clone.1 | convolution fusion | flops 14942208 | bytes 5281792 | tf_op jit(solution)/shard_map/while/body/eval_jaxpr/ia,ipa->ip/dot_general | solution.py:70
  576.6 11.9 %fusion.328 = f32[512,1,19]{2,1,0:T(1,128)S(1)} fusion(f32[512,128,1]{1,2,0:T(1,128)S(1)} %bitcast.372, f32[512,19,128]{2,0,1:T(8,128)S(1)} %fusion.327), kind=kOutput, calls=%fused_computation.94.clone.1 | convolution fusion | flops 14942208 | bytes 5281792 | tf_op jit(solution)/shard_map/while/body/eval_jaxpr/ia,ipa->ip/dot_general | solution.py:73
  594.5 12.1 %fusion.329 = f32[512,1,19]{2,1,0:T(1,128)S(1)} fusion(f32[512,128,1]{1,2,0:T(1,128)S(1)} %bitcast.379, f32[512,19,128]{2,0,1:T(8,128)S(1)} %fusion.325), kind=kOutput, calls=%fused_computation.92.clone.1 | convolution fusion | flops 14942208 | bytes 5281792 | tf_op jit(solution)/shard_map/while/body/eval_jaxpr/ia,ipa->ip/dot_general | solution.py:71
  606.6 11.9 %fusion.326 = f32[512,1,19]{2,1,0:T(1,128)S(1)} fusion(f32[512,128,1]{1,2,0:T(1,128)S(1)} %bitcast.373, f32[512,19,128]{2,0,1:T(8,128)S(1)} %fusion.325), kind=kOutput, calls=%fused_computation.90.clone.1 | convolution fusion | flops 14942208 | bytes 5281792 | tf_op jit(solution)/shard_map/while/body/eval_jaxpr/ia,ipa->ip/dot_general | solution.py:70
  622.5 14.6 %all-reduce.1 = (f32[4]{0:T(128)S(1)}, f32[4]{0:T(128)S(1)}) all-reduce(f32[4]{0:T(128)S(1)} %broadcast_multiply_fusion.2, f32[4]{0:T(128)S(1)} %get-tuple-element.210), channel_id=1, replica_groups=mesh['win'=4,'slab'=8] {'slab'}, use_global_device_ids=true, to_apply=%region_6.7 | all-reduce | flops 8 | bytes 64 | tf_op jit(solution)/shard_map/psum | solution.py:204
  (170 shorter events, 221.0 us)
Async XLA Ops:
  28.4 20.9 %copy-start.4 = (f32[4,512]{1,0:T(4,128)}, f32[4,512]{1,0:T(4,128)S(1)}, u32[]{:S(2)}) copy-start(f32[4,512]{1,0:T(4,128)S(1)} %get-tuple-element.728) | copy-start | bytes 24580
  29.6 13.6 %collective-permute-start = (f32[4,3,128,128]{2,3,1,0:T(8,128)S(1)}, f32[4,3,128,128]{2,3,1,0:T(8,128)S(1)}, u32[]{:S(2)}, u32[]{:S(2)}) collective-permute-start(f32[4,3,128,128]{2,3,1,0:T(8,128)S(1)} %slice.373), channel_id=1, source_target_pairs={{0,1},{1,2},{2,3},{3,4},{4,5},{5,6},{6,7},{7,0},{8,9},{9,10},{10,1... | collective-permute-start | bytes 2359304 | tf_op jit(solution)/shard_map/ppermute | solution.py:17
  49.3 14.4 %slice-start = ((s8[4980736]{0:T(1024)(128)(4,1)}), s8[4194304]{0:T(1024)(128)(4,1)S(1)}, s32[]{:S(2)}) async-start(s8[4980736]{0:T(1024)(128)(4,1)} %bitcast.380), calls=%async_computation.2 | async-start | bytes 8388608
  56.2 7.5 %slice-start.1 = ((s8[4980736]{0:T(1024)(128)(4,1)}), s8[786432]{0:T(1024)(128)(4,1)S(1)}, s32[]{:S(2)}) async-start(s8[4980736]{0:T(1024)(128)(4,1)} %bitcast.380), calls=%async_computation.3 | async-start | bytes 1572864
  91.4 99.2 %all-to-all-start = ((f32[4,2,16,128,128]{4,2,0,1,3:T(8,128)}), f32[4,2,16,128,128]{4,2,0,1,3:T(8,128)}, u32[]{:S(2)}, u32[]{:S(2)}) async-start(f32[4,2,16,128,128]{4,2,0,1,3:T(8,128)} %copy.64), calls=%async_computation | async-start | bytes 16777216 | tf_op jit(solution)/shard_map/all_to_all | solution.py:179
  208.0 7.3 %copy-start.1 = (f32[4,1,128,16,128]{2,4,3,0,1:T(8,128)S(1)}, f32[4,1,128,16,128]{2,4,3,0,1:T(8,128)}, u32[]{:S(2)}) copy-start(f32[4,1,128,16,128]{2,4,3,0,1:T(8,128)} %copy.119) | copy-start | bytes 12582916
  236.8 4.0 copy-start
  236.8 4.0 copy-start.3
  389.9 9.2 %copy-start.5 = (f32[3,4,4,512]{3,2,1,0:T(4,128)S(1)}, f32[3,4,4,512]{3,2,1,0:T(4,128)}, u32[]{:S(2)}) copy-start(f32[3,4,4,512]{3,2,1,0:T(4,128)} %param.17) | copy-start | bytes 294916
  396.9 2.0 copy-start.2
  399.0 9.6 %collective-permute-start.1 = (f32[4,3,128,128]{2,3,1,0:T(8,128)S(1)}, f32[4,3,128,128]{2,3,1,0:T(8,128)S(1)}, u32[]{:S(2)}, u32[]{:S(2)}) collective-permute-start(f32[4,3,128,128]{2,3,1,0:T(8,128)S(1)} %slice.383), channel_id=1, source_target_pairs={{0,7},{1,0},{2,1},{3,2},{4,3},{5,4},{6,5},{7,6},{8,15},{9,8},{10,9... | collective-permute-start | bytes 2359304 | tf_op jit(solution)/shard_map/ppermute | solution.py:17
  622.5 15.1 %copy-start.6 = (f32[4,3,512]{2,0,1:T(4,128)}, f32[4,3,512]{2,0,1:T(4,128)S(1)}, u32[]{:S(2)}) copy-start(f32[4,3,512]{2,0,1:T(4,128)S(1)} %get-tuple-element.209) | copy-start | bytes 73732
where the time goes:
time: 644 us; the launch traced here: 638 us
  matrix products  322 us (50%)
  waiting for transfers between devices  115 us (18%)
  blocking collectives  112 us (17%)
  local copies, waits for them, and re-layouts  52.8 us (8%)
  other arithmetic  25.1 us (4%)
    all_to_all x1, blocking collectives, body(): lax.all_to_all(stacked, 'slab', split_axis=2, concat_axis=3, tiled=True)  97.8 us
    all_to_all x1, waiting for transfers between devices, body(): lax.all_to_all(slab_spectrum, 'slab', split_axis=3, concat_axis=2, tiled=...  93.5 us
    dot_general x4, matrix products, sample_block(): jnp.einsum('ia,ipa->ip', steep_x, along_rows, precision=highest)  48 us
    dot_general x4, matrix products, sample_block(): jnp.einsum('ia,ipa->ip', rows_x, along_steep, precision=highest)  47.8 us
    dot_general x4, matrix products, sample_block(): reduced = jnp.einsum('ia,ipa->ip', rows_x, along_rows, precision=highest)  47.8 us
    dot_general x4, matrix products, sample_block(): along_steep = jnp.einsum('pab,ib->ipa', values, steep_y, precision=highest)  23.8 us
    dot_general x4, matrix products, sample_block(): along_rows = jnp.einsum('pab,ib->ipa', values, rows_y, precision=highest)  23.8 us
    ppermute x2, waiting for transfers between devices, passed_along(): return lax.ppermute(value, axis, pairs)  22 us
  transfers between devices with their start and end apart: 3, of which 3 were waited for; matrix products, arithmetic and copies ran while one was open for 0% of the time, Pallas kernels for 0%

commit v1 on v0

--- a/solution.py
+++ b/solution.py
@@ -9,6 +9,22 @@
 NZ = 128
 highest = lax.Precision.HIGHEST
 gauss_width = 2.0
+
+
+def pairwise_exchange(value, axis, split, join):
+    ways, here = (lax.axis_size(axis), lax.axis_index(axis))
+    width = value.shape[split] // ways
+    shape = list(value.shape)
+    shape[split] = width
+    height = shape[join]
+    shape[join] = height * ways
+    full = jnp.zeros(shape, value.dtype)
+    for mask in range(ways):
+        part = lax.dynamic_slice_in_dim(value, (here ^ mask) * width, width, axis=split)
+        if mask:
+            part = lax.ppermute(part, axis, [(d, d ^ mask) for d in range(ways)])
+        full = lax.dynamic_update_slice_in_dim(full, part, (here ^ mask) * height, axis=join)
+    return full
 
 
 def passed_along(value, axis, steps):
@@ -176,10 +192,7 @@
     slab_spectrum = xy_forward(owned_grid, planar)
     influence = influence_block(lax.axis_index("slab") * column_count, column_count)
     stacked, energy_part = column_transform(
-        lax.all_to_all(slab_spectrum, "slab", split_axis=3, concat_axis=2, tiled=True),
-        influence,
-        cosine_z,
-        sine_z,
+        pairwise_exchange(slab_spectrum, "slab", 3, 2), influence, cosine_z, sine_z
     )
     slab_values = lax.all_to_all(stacked, "slab", split_axis=2, concat_axis=3, tiled=True)
     slab_values, energy_part = (slab_values, energy_part)

time: 644 us -> 1010 us (1.57)
  local copies, waits for them, and re-layouts: 52.8 us -> 480 us
  waiting for transfers between devices: 115 us -> 39.4 us
    dynamic_update_slice x0 -> x8, local copies, waits for them, and re-layouts: none -> 404 us  [pairwise_exchange(): lax.dynamic_update_slice_in_dim(full, part, (here ^ mask) * height, axis=...]
    all_to_all x1 -> x0, waiting for transfers between devices: 93.5 us -> none  [body(): lax.all_to_all(slab_spectrum, 'slab', split_axis=3, concat_axis=2, tiled=...]
    ppermute x0 -> x7, local copies, waits for them, and re-layouts: none -> 39.2 us  [pairwise_exchange(): part = lax.ppermute(part, axis, [(d, d ^ mask) for d in range(ways)])]
    ppermute x0 -> x7, waiting for transfers between devices: none -> 17.4 us  [pairwise_exchange(): part = lax.ppermute(part, axis, [(d, d ^ mask) for d in range(ways)])]
  transfers between devices with their start and end apart: 3 -> 9, of which waited for: 3 -> 3; matrix products, arithmetic and copies ran while one was open for 0% -> 40% of each run, Pallas kernels for 0% -> 0%
where the time goes in v1:
time: 1010 us; the launch traced here: 995 us
  local copies, waits for them, and re-layouts  480 us (48%)
  matrix products  317 us (31%)
  blocking collectives  112 us (11%)
  waiting for transfers between devices  39.4 us (4%)
  other arithmetic  34 us (3%)
    dynamic_update_slice x8, local copies, waits for them, and re-layouts, pairwise_exchange(): lax.dynamic_update_slice_in_dim(full, part, (here ^ mask) * height, axis=...  404 us
    all_to_all x1, blocking collectives, body(): lax.all_to_all(stacked, 'slab', split_axis=2, concat_axis=3, tiled=True)  97.8 us
    dot_general x4, matrix products, sample_block(): jnp.einsum('ia,ipa->ip', steep_x, along_rows, precision=highest)  48 us
    dot_general x4, matrix products, sample_block(): jnp.einsum('ia,ipa->ip', rows_x, along_steep, precision=highest)  47.8 us
    dot_general x4, matrix products, sample_block(): reduced = jnp.einsum('ia,ipa->ip', rows_x, along_rows, precision=highest)  47.8 us
    ppermute x7, local copies, waits for them, and re-layouts, pairwise_exchange(): part = lax.ppermute(part, axis, [(d, d ^ mask) for d in range(ways)])  39.2 us
    dot_general x4, matrix products, sample_block(): along_steep = jnp.einsum('pab,ib->ipa', values, steep_y, precision=highest)  23.8 us
    dot_general x4, matrix products, sample_block(): along_rows = jnp.einsum('pab,ib->ipa', values, rows_y, precision=highest)  23.8 us
  transfers between devices with their start and end apart: 9, of which 3 were waited for; matrix products, arithmetic and copies ran while one was open for 40% of the time, Pallas kernels for 0%

profile of v1, /device:TPU:0, one launch (start us, length us, event | category | flops | bytes accessed | tf_op | source)
XLA Modules:
  0.0 994.8 jit_solution(9527563143507040582)
XLA Ops:
  3.7 25.2 %while.26 = (s32[]{:T(128)}, f32[4,19,128,128]{2,3,1,0:T(8,128)}, s32[4,3,512]{2,1,0:T(4,128)S(1)}, s32[]{:T(128)}, f32[4,3,4,512]{3,2,1,0:T(4,128)S(1)}, /*inde...) while((s32[]{:T(128)}, f32[4,19,128,128]{2,3,1,0:T(8,128)}, ...), condition=%wide.region_1.2_spmd, body=%wide.region_0.1_spmd.sunk | while | flops 1915456512 | bytes 2517685 | solution.py:183
  31.8 12.5 %collective-permute-done = f32[4,3,128,128]{2,3,1,0:T(8,128)S(1)} collective-permute-done((f32[4,3,128,128]{2,3,1,0:T(8,128)S(1)}, f32[4,3,128,128]{2,3,1,0:T(8,128)S(1)}, u32[]{:S(2)}, u32[]{:S(2)}) %collective-permute-start) | collective-permute-done | bytes 786464 | tf_op jit(solution)/shard_map/ppermute | solution.py:33
  96.0 17.4 %collective-permute-done.2 = f32[4,2,16,16,128]{4,3,2,0,1:T(8,128)S(1)} collective-permute-done((f32[4,2,16,16,128]{4,3,2,0,1:T(8,128)}, f32[4,2,16,16,128]{4,3,2,0,1:T(8,128)S(1)}, u32[]{:S(2)}, u32[]{:S(2)}) %collective-permute-start.2) | collective-permute-done | bytes 1048608 | tf_op jit(solution)/shard_map/ppermute | solution.py:25
  124.0 39.3 %dynamic_update_slice.45 = f32[4,2,128,16,128]{2,4,3,0,1:T(8,128)} dynamic-update-slice(f32[4,2,128,16,128]{2,4,3,0,1:T(8,128)} %broadcast_in_dim.30, f32[4,2,16,16,128]{2,4,3,0,1:T(8,128)} %copy.56, s32[]{:T(128)} %constant.329.clone.1, s32[]{:T(128)} %constant.329.clone.1, s32[]{:T(128)S(6)} %select_n.322, s32[]{:T(128)} %constant.329.clone.1, s32[]{:T(128)} %constant.329.clone.1) | dynamic-update-slice | bytes 2097156 | tf_op jit(solution)/shard_map/dynamic_update_slice | solution.py:26
  167.9 52.2 %dynamic_update_slice.46 = f32[4,2,128,16,128]{2,4,3,0,1:T(8,128)} dynamic-update-slice(f32[4,2,128,16,128]{2,4,3,0,1:T(8,128)} %dynamic_update_slice.45, f32[4,2,16,16,128]{2,4,3,0,1:T(8,128)} %copy.57, s32[]{:T(128)} %constant.329.clone.1, s32[]{:T(128)} %constant.329.clone.1, s32[]{:T(128)S(6)} %select_n.323, s32[]{:T(128)} %constant.329.clone.1, s32[]{:T(128)} %constant.329.clone.1) | dynamic-update-slice | bytes 2097156 | tf_op jit(solution)/shard_map/dynamic_update_slice | solution.py:26
  224.7 52.2 %dynamic_update_slice.47 = f32[4,2,128,16,128]{2,4,3,0,1:T(8,128)} dynamic-update-slice(f32[4,2,128,16,128]{2,4,3,0,1:T(8,128)} %dynamic_update_slice.46, f32[4,2,16,16,128]{2,4,3,0,1:T(8,128)} %copy.58, s32[]{:T(128)} %constant.329.clone.1, s32[]{:T(128)} %constant.329.clone.1, s32[]{:T(128)S(6)} %select_n.324, s32[]{:T(128)} %constant.329.clone.1, s32[]{:T(128)} %constant.329.clone.1) | dynamic-update-slice | bytes 2097156 | tf_op jit(solution)/shard_map/dynamic_update_slice | solution.py:26
  282.9 52.2 %dynamic_update_slice.48 = f32[4,2,128,16,128]{2,4,3,0,1:T(8,128)} dynamic-update-slice(f32[4,2,128,16,128]{2,4,3,0,1:T(8,128)} %dynamic_update_slice.47, f32[4,2,16,16,128]{2,4,3,0,1:T(8,128)} %copy.59, s32[]{:T(128)} %constant.329.clone.1, s32[]{:T(128)} %constant.329.clone.1, s32[]{:T(128)S(6)} %select_n.325, s32[]{:T(128)} %constant.329.clone.1, s32[]{:T(128)} %constant.329.clone.1) | dynamic-update-slice | bytes 2097156 | tf_op jit(solution)/shard_map/dynamic_update_slice | solution.py:26
  341.0 52.2 %dynamic_update_slice.49 = f32[4,2,128,16,128]{2,4,3,0,1:T(8,128)} dynamic-update-slice(f32[4,2,128,16,128]{2,4,3,0,1:T(8,128)} %dynamic_update_slice.48, f32[4,2,16,16,128]{2,4,3,0,1:T(8,128)} %copy.60, s32[]{:T(128)} %constant.329.clone.1, s32[]{:T(128)} %constant.329.clone.1, s32[]{:T(128)S(6)} %select_n.326, s32[]{:T(128)} %constant.329.clone.1, s32[]{:T(128)} %constant.329.clone.1) | dynamic-update-slice | bytes 2097156 | tf_op jit(solution)/shard_map/dynamic_update_slice | solution.py:26
  399.2 52.2 %dynamic_update_slice.50 = f32[4,2,128,16,128]{2,4,3,0,1:T(8,128)} dynamic-update-slice(f32[4,2,128,16,128]{2,4,3,0,1:T(8,128)} %dynamic_update_slice.49, f32[4,2,16,16,128]{2,4,3,0,1:T(8,128)} %copy.61, s32[]{:T(128)} %constant.329.clone.1, s32[]{:T(128)} %constant.329.clone.1, s32[]{:T(128)S(6)} %select_n.327, s32[]{:T(128)} %constant.329.clone.1, s32[]{:T(128)} %constant.329.clone.1) | dynamic-update-slice | bytes 2097156 | tf_op jit(solution)/shard_map/dynamic_update_slice | solution.py:26
  457.3 52.2 %dynamic_update_slice.51 = f32[4,2,128,16,128]{2,4,3,0,1:T(8,128)} dynamic-update-slice(f32[4,2,128,16,128]{2,4,3,0,1:T(8,128)} %dynamic_update_slice.50, f32[4,2,16,16,128]{2,4,3,0,1:T(8,128)} %copy.62, s32[]{:T(128)} %constant.329.clone.1, s32[]{:T(128)} %constant.329.clone.1, s32[]{:T(128)S(6)} %select_n.328, s32[]{:T(128)} %constant.329.clone.1, s32[]{:T(128)} %constant.329.clone.1) | dynamic-update-slice | bytes 2097156 | tf_op jit(solution)/shard_map/dynamic_update_slice | solution.py:26
  515.5 52.2 %dynamic_update_slice.52 = f32[4,2,128,16,128]{2,4,3,0,1:T(8,128)} dynamic-update-slice(f32[4,2,128,16,128]{2,4,3,0,1:T(8,128)} %dynamic_update_slice.51, f32[4,2,16,16,128]{2,4,3,0,1:T(8,128)} %copy.63, s32[]{:T(128)} %constant.329.clone.1, s32[]{:T(128)} %constant.329.clone.1, s32[]{:T(128)S(6)} %select_n.329, s32[]{:T(128)} %constant.329.clone.1, s32[]{:T(128)} %constant.329.clone.1) | dynamic-update-slice | bytes 2097156 | tf_op jit(solution)/shard_map/dynamic_update_slice | solution.py:26
  616.9 97.8 %all_to_all.18 = f32[4,2,128,16,128]{4,3,0,1,2:T(8,128)S(1)} all-to-all(f32[4,2,128,16,128]{4,3,0,1,2:T(8,128)} %copy.64), channel_id=1, replica_groups=mesh['win'=4,'slab'=8] {'slab'}, dimensions={2} | all-to-all | bytes 16777216 | tf_op jit(solution)/shard_map/all_to_all | solution.py:197
  762.9 216.4 %while.27 = (s32[]{:T(128)}, f32[4,3,512]{2,0,1:T(4,128)S(1)}, f32[4]{0:T(128)S(1)}, f32[4,512]{1,0:T(4,128)}, s32[4,3,512]{2,1,0:T(4,128)}, /*index=5*/s32[]{:T...) while((s32[]{:T(128)}, f32[4,3,512]{2,0,1:T(4,128)S(1)}, ...), condition=%wide.region_4.5_spmd, body=%wide.region_2.4_spmd.sunk | while | flops 3872960512 | bytes 29543656 | solution.py:212
  771.8 11.9 %fusion.327 = f32[512,1,19]{2,1,0:T(1,128)S(1)} fusion(f32[512,128,1]{1,2,0:T(1,128)S(1)} %bitcast.366, f32[512,19,128]{2,0,1:T(8,128)S(1)} %fusion.326), kind=kOutput, calls=%fused_computation.94.clone.1 | convolution fusion | flops 14942208 | bytes 5281792 | tf_op jit(solution)/shard_map/while/body/eval_jaxpr/ia,ipa->ip/dot_general | solution.py:89
  789.7 12.1 %fusion.328 = f32[512,1,19]{2,1,0:T(1,128)S(1)} fusion(f32[512,128,1]{1,2,0:T(1,128)S(1)} %bitcast.372, f32[512,19,128]{2,0,1:T(8,128)S(1)} %fusion.324), kind=kOutput, calls=%fused_computation.92.clone.1 | convolution fusion | flops 14942208 | bytes 5281792 | tf_op jit(solution)/shard_map/while/body/eval_jaxpr/ia,ipa->ip/dot_general | solution.py:87
  801.8 11.9 %fusion.325 = f32[512,1,19]{2,1,0:T(1,128)S(1)} fusion(f32[512,128,1]{1,2,0:T(1,128)S(1)} %bitcast.367, f32[512,19,128]{2,0,1:T(8,128)S(1)} %fusion.324), kind=kOutput, calls=%fused_computation.90.clone.1 | convolution fusion | flops 14942208 | bytes 5281792 | tf_op jit(solution)/shard_map/while/body/eval_jaxpr/ia,ipa->ip/dot_general | solution.py:86
  825.6 12.1 %fusion.327 = f32[512,1,19]{2,1,0:T(1,128)S(1)} fusion(f32[512,128,1]{1,2,0:T(1,128)S(1)} %bitcast.366, f32[512,19,128]{2,0,1:T(8,128)S(1)} %fusion.326), kind=kOutput, calls=%fused_computation.94.clone.1 | convolution fusion | flops 14942208 | bytes 5281792 | tf_op jit(solution)/shard_map/while/body/eval_jaxpr/ia,ipa->ip/dot_general | solution.py:89
  843.7 11.9 %fusion.328 = f32[512,1,19]{2,1,0:T(1,128)S(1)} fusion(f32[512,128,1]{1,2,0:T(1,128)S(1)} %bitcast.372, f32[512,19,128]{2,0,1:T(8,128)S(1)} %fusion.324), kind=kOutput, calls=%fused_computation.92.clone.1 | convolution fusion | flops 14942208 | bytes 5281792 | tf_op jit(solution)/shard_map/while/body/eval_jaxpr/ia,ipa->ip/dot_general | solution.py:87
  855.5 11.9 %fusion.325 = f32[512,1,19]{2,1,0:T(1,128)S(1)} fusion(f32[512,128,1]{1,2,0:T(1,128)S(1)} %bitcast.367, f32[512,19,128]{2,0,1:T(8,128)S(1)} %fusion.324), kind=kOutput, calls=%fused_computation.90.clone.1 | convolution fusion | flops 14942208 | bytes 5281792 | tf_op jit(solution)/shard_map/while/body/eval_jaxpr/ia,ipa->ip/dot_general | solution.py:86
  897.4 11.9 %fusion.328 = f32[512,1,19]{2,1,0:T(1,128)S(1)} fusion(f32[512,128,1]{1,2,0:T(1,128)S(1)} %bitcast.372, f32[512,19,128]{2,0,1:T(8,128)S(1)} %fusion.324), kind=kOutput, calls=%fused_computation.92.clone.1 | convolution fusion | flops 14942208 | bytes 5281792 | tf_op jit(solution)/shard_map/while/body/eval_jaxpr/ia,ipa->ip/dot_general | solution.py:87
  909.3 12.1 %fusion.325 = f32[512,1,19]{2,1,0:T(1,128)S(1)} fusion(f32[512,128,1]{1,2,0:T(1,128)S(1)} %bitcast.367, f32[512,19,128]{2,0,1:T(8,128)S(1)} %fusion.324), kind=kOutput, calls=%fused_computation.90.clone.1 | convolution fusion | flops 14942208 | bytes 5281792 | tf_op jit(solution)/shard_map/while/body/eval_jaxpr/ia,ipa->ip/dot_general | solution.py:86
  933.3 11.9 %fusion.327 = f32[512,1,19]{2,1,0:T(1,128)S(1)} fusion(f32[512,128,1]{1,2,0:T(1,128)S(1)} %bitcast.366, f32[512,19,128]{2,0,1:T(8,128)S(1)} %fusion.326), kind=kOutput, calls=%fused_computation.94.clone.1 | convolution fusion | flops 14942208 | bytes 5281792 | tf_op jit(solution)/shard_map/while/body/eval_jaxpr/ia,ipa->ip/dot_general | solution.py:89
  951.2 12.1 %fusion.328 = f32[512,1,19]{2,1,0:T(1,128)S(1)} fusion(f32[512,128,1]{1,2,0:T(1,128)S(1)} %bitcast.372, f32[512,19,128]{2,0,1:T(8,128)S(1)} %fusion.324), kind=kOutput, calls=%fused_computation.92.clone.1 | convolution fusion | flops 14942208 | bytes 5281792 | tf_op jit(solution)/shard_map/while/body/eval_jaxpr/ia,ipa->ip/dot_general | solution.py:87
  979.4 14.6 %all-reduce.1 = (f32[4]{0:T(128)S(1)}, f32[4]{0:T(128)S(1)}) all-reduce(f32[4]{0:T(128)S(1)} %broadcast_multiply_fusion.2, f32[4]{0:T(128)S(1)} %get-tuple-element.210), channel_id=1, replica_groups=mesh['win'=4,'slab'=8] {'slab'}, use_global_device_ids=true, to_apply=%region_6.7 | all-reduce | flops 8 | bytes 64 | tf_op jit(solution)/shard_map/psum | solution.py:217
  (203 shorter events, 324.4 us)
Async XLA Ops:
  28.9 0.6 copy-start.4
  28.9 0.7 copy-start.7
  28.9 0.7 copy-start.8
  30.8 13.6 %collective-permute-start = (f32[4,3,128,128]{2,3,1,0:T(8,128)S(1)}, f32[4,3,128,128]{2,3,1,0:T(8,128)S(1)}, u32[]{:S(2)}, u32[]{:S(2)}) collective-permute-start(f32[4,3,128,128]{2,3,1,0:T(8,128)S(1)} %slice.373), channel_id=1, source_target_pairs={{0,1},{1,2},{2,3},{3,4},{4,5},{5,6},{6,7},{7,0},{8,9},{9,10},{10,1... | collective-permute-start | bytes 2359304 | tf_op jit(solution)/shard_map/ppermute | solution.py:33
  50.4 14.2 %slice-start = ((s8[4980736]{0:T(1024)(128)(4,1)}), s8[4194304]{0:T(1024)(128)(4,1)S(1)}, s32[]{:S(2)}) async-start(s8[4980736]{0:T(1024)(128)(4,1)} %bitcast.373), calls=%async_computation.1 | async-start | bytes 8388608
  57.4 7.3 slice-start.1
  75.9 7.6 copy-start.1
  83.5 3.6 copy-start.2
  87.1 7.2 collective-permute-start.1
  87.1 26.2 %collective-permute-start.2 = (f32[4,2,16,16,128]{4,3,2,0,1:T(8,128)}, f32[4,2,16,16,128]{4,3,2,0,1:T(8,128)S(1)}, u32[]{:S(2)}, u32[]{:S(2)}) collective-permute-start(f32[4,2,16,16,128]{4,3,2,0,1:T(8,128)} %get-tuple-element.375), channel_id=1, source_target_pairs={{0,2},{1,3},{2,0},{3,1},{4,6},{5,7},{6,4},{7,5},{8,10},{9,11},{10,... | collective-permute-start | bytes 3145736 | tf_op jit(solution)/shard_map/ppermute | solution.py:25
  88.4 188.4 %collective-permute-start.3 = (f32[4,2,16,16,128]{4,3,2,0,1:T(8,128)}, f32[4,2,16,16,128]{4,3,2,0,1:T(8,128)}, u32[]{:S(2)}, u32[]{:S(2)}) collective-permute-start(f32[4,2,16,16,128]{4,3,2,0,1:T(8,128)} %get-tuple-element.376), channel_id=1, source_target_pairs={{0,3},{1,2},{2,1},{3,0},{4,7},{5,6},{6,5},{7,4},{8,11},{9,10},{10,... | collective-permute-start | bytes 3145736 | tf_op jit(solution)/shard_map/ppermute | solution.py:25
  88.9 246.1 %collective-permute-start.4 = (f32[4,2,16,16,128]{4,3,2,0,1:T(8,128)}, f32[4,2,16,16,128]{4,3,2,0,1:T(8,128)}, u32[]{:S(2)}, u32[]{:S(2)}) collective-permute-start(f32[4,2,16,16,128]{4,3,2,0,1:T(8,128)} %get-tuple-element.377), channel_id=1, source_target_pairs={{0,4},{1,5},{2,6},{3,7},{4,0},{5,1},{6,2},{7,3},{8,12},{9,13},{10,... | collective-permute-start | bytes 3145736 | tf_op jit(solution)/shard_map/ppermute | solution.py:25
  94.3 298.9 %collective-permute-start.5 = (f32[4,2,16,16,128]{4,3,2,0,1:T(8,128)}, f32[4,2,16,16,128]{4,3,2,0,1:T(8,128)}, u32[]{:S(2)}, u32[]{:S(2)}) collective-permute-start(f32[4,2,16,16,128]{4,3,2,0,1:T(8,128)} %get-tuple-element.379), channel_id=1, source_target_pairs={{0,5},{1,4},{2,7},{3,6},{4,1},{5,0},{6,3},{7,2},{8,13},{9,12},{10,... | collective-permute-start | bytes 3145736 | tf_op jit(solution)/shard_map/ppermute | solution.py:25
  94.3 20.3 %copy-start.5 = (f32[4,2,16,16,128]{4,3,2,0,1:T(8,128)}, f32[4,2,16,16,128]{4,3,2,0,1:T(8,128)S(1)}, u32[]{:S(2)}) copy-start(f32[4,2,16,16,128]{4,3,2,0,1:T(8,128)S(1)} %collective-permute-done.1) | copy-start | bytes 3145732
  94.3 357.0 %collective-permute-start.6 = (f32[4,2,16,16,128]{4,3,2,0,1:T(8,128)}, f32[4,2,16,16,128]{4,3,2,0,1:T(8,128)}, u32[]{:S(2)}, u32[]{:S(2)}) collective-permute-start(f32[4,2,16,16,128]{4,3,2,0,1:T(8,128)} %get-tuple-element.378), channel_id=1, source_target_pairs={{0,6},{1,7},{2,4},{3,5},{4,2},{5,3},{6,0},{7,1},{8,14},{9,15},{10,... | collective-permute-start | bytes 3145736 | tf_op jit(solution)/shard_map/ppermute | solution.py:25
  113.3 396.1 %collective-permute-start.7 = (f32[4,2,16,16,128]{4,3,2,0,1:T(8,128)}, f32[4,2,16,16,128]{4,3,2,0,1:T(8,128)}, u32[]{:S(2)}, u32[]{:S(2)}) collective-permute-start(f32[4,2,16,16,128]{4,3,2,0,1:T(8,128)} %get-tuple-element.372), channel_id=1, source_target_pairs={{0,7},{1,6},{2,5},{3,4},{4,3},{5,2},{6,1},{7,0},{8,15},{9,14},{10,... | collective-permute-start | bytes 3145736 | tf_op jit(solution)/shard_map/ppermute | solution.py:25
  124.0 39.3 %copy-start.6 = (f32[4,2,16,16,128]{4,3,2,0,1:T(8,128)S(1)}, f32[4,2,16,16,128]{4,3,2,0,1:T(8,128)}, u32[]{:S(2)}) copy-start(f32[4,2,16,16,128]{4,3,2,0,1:T(8,128)} %copy-done.5) | copy-start | bytes 3145732
  567.6 6.2 copy-start
  738.9 9.6 copy-start.9
  745.9 2.0 copy-start.3
  748.0 10.0 %collective-permute-start.8 = (f32[4,3,128,128]{2,3,1,0:T(8,128)S(1)}, f32[4,3,128,128]{2,3,1,0:T(8,128)S(1)}, u32[]{:S(2)}, u32[]{:S(2)}) collective-permute-start(f32[4,3,128,128]{2,3,1,0:T(8,128)S(1)} %slice.383), channel_id=1, source_target_pairs={{0,7},{1,0},{2,1},{3,2},{4,3},{5,4},{6,5},{7,6},{8,15},{9,8},{10,9... | collective-permute-start | bytes 2359304 | tf_op jit(solution)/shard_map/ppermute | solution.py:33
  979.4 15.1 %copy-start.10 = (f32[4,3,512]{2,0,1:T(4,128)}, f32[4,3,512]{2,0,1:T(4,128)S(1)}, u32[]{:S(2)}) copy-start(f32[4,3,512]{2,0,1:T(4,128)S(1)} %get-tuple-element.209) | copy-start | bytes 73732
